TPU v7x, 32 devices: a whole 2x2x4 slice. The times are simulated.
32 devices in a mesh: gx: 8 (over z, y), gy: 4 (over x, core).
Axes of the slice: x: 2, y: 2, z: 4, core: 2. Of those that a mesh axis runs over, the one named last changes fastest.
Arguments:
- goal_embed: bfloat16 [4096, 128], P(('gx', 'gy')), may hold values from -6 to 6
- goal_bins: int32 [4096], P(('gx', 'gy')), may hold values from 0 to 2047, as said below
- goal_weights: float32 [4096], P(('gx', 'gy')), may hold values from 0.1 to 10
Outputs:
- bin_mean: float32 [2048, 128], P(('gx', 'gy'))
- rarity: float32 [2048], P(('gx', 'gy'))
Inputs may be any that keep to these rules, and one draw needn't show every extreme that they name: `goal_bins`: bin b belongs to owner b // 64, owners numbered in the order of gx then gy. Of the goals of one device, at most 8 fall in the bins of one owner; some owner receives exactly 8 goals from every device.
All inputs are finite; a program needn't handle non-finite values.
Results may differ from a plain program's by a relative error of at most 0.0029.
Values may be sent and summed in bfloat16 or wider, within the bound.
A program may use at most 64 MiB of HBM per device.

v0:
```python
import jax
import jax.numpy as jnp
from jax import lax
from jax.sharding import PartitionSpec as P

BINS_DEV = 64


def shards(goal_embed, goal_bins, goal_weights):
    scaled = (goal_weights[:, None] * goal_embed.astype(jnp.float32)).astype(jnp.bfloat16)
    width = goal_embed.shape[1]
    local_goals = goal_embed.shape[0]
    across = lax.axis_size("gx")
    along = lax.axis_size("gy")
    devices = across * along
    capacity = max(2, 2 * local_goals // devices)
    owners = goal_bins // BINS_DEV
    offsets = goal_bins - owners * BINS_DEV
    member = (owners[:, None] == jnp.arange(devices, dtype=jnp.int32)[None, :]).astype(jnp.int32)
    before = jnp.cumsum(member, axis=0) - member
    places = jnp.sum(before * member, axis=1)
    slots = owners * capacity + places
    outgoing = jnp.zeros((devices * capacity, width), jnp.bfloat16).at[slots].set(scaled)
    tagging = jnp.zeros((2, devices * capacity), jnp.float32)
    tagging = tagging.at[0, slots].set(goal_weights).at[1, slots].set(offsets.astype(jnp.float32))
    outgoing = outgoing.reshape(across, along, capacity, width)
    tagging = tagging.reshape(2, across, along, capacity)
    arrived = lax.all_to_all(
        lax.all_to_all(outgoing, "gx", split_axis=0, concat_axis=0, tiled=True),
        "gy",
        split_axis=1,
        concat_axis=1,
        tiled=True,
    )
    tag_rows = lax.all_to_all(
        lax.all_to_all(tagging, "gx", split_axis=1, concat_axis=1, tiled=True),
        "gy",
        split_axis=2,
        concat_axis=2,
        tiled=True,
    )
    arrived = arrived.reshape(devices * capacity, width)
    tag_rows = tag_rows.reshape(2, devices * capacity)
    labels = lax.broadcasted_iota(jnp.int32, (BINS_DEV, 1), 0).astype(jnp.float32)
    selector = tag_rows[1][None, :] == labels
    bin_sums = jnp.dot(selector.astype(jnp.bfloat16), arrived, preferred_element_type=jnp.float32)
    bin_mass = jnp.dot(selector.astype(jnp.float32), tag_rows[0], precision=lax.Precision.HIGHEST)
    total_mass = lax.psum(jnp.sum(bin_mass), ("gx", "gy"))
    bin_mean = bin_sums / (bin_mass[:, None] + 1.0)
    rarity = jnp.log(total_mass / (BINS_DEV * devices)) - jnp.log(bin_mass + 1.0)
    return (bin_mean, rarity)


def solution(mesh):
    in_specs = (P(("gx", "gy"), None), P(("gx", "gy")), P(("gx", "gy")))
    out_specs = (P(("gx", "gy"), None), P(("gx", "gy")))
    return jax.shard_map(shards, mesh=mesh, in_specs=in_specs, out_specs=out_specs, check_vma=False)
```

profile of v0, /device:TPU:0, one launch (start us, length us, event | category | flops | bytes accessed | tf_op | source)
XLA Modules:
  0.0 93.1 jit_solution(4781643750971819764)
XLA Ops:
  0.6 0.7 subtract_convert_fusion
  1.3 0.1 fusion.2
  1.4 0.2 reduce_window_sum.11
  1.6 0.2 select_reduce_fusion
  1.8 0.0 copy-start.1
  1.8 0.6 copy-done.1
  2.4 6.9 %scatter_fusion = f32[2,256]{1,0:T(2,128)S(1)} fusion(f32[2,256]{1,0:T(2,128)S(1)} %broadcast_in_dim.6, s32[128]{0:T(128)S(1)} %select_bitcast_fusion.1, f32[128]{0:T(128)S(1)} %copy-done.1), kind=kCustom, calls=%fused_computation | custom fusion | bytes 2560 | tf_op jit(solution)/shard_map/scatter | solution.py:25
  9.3 6.9 %scatter_fusion.1 = f32[2,256]{1,0:T(2,128)S(1)} fusion(f32[2,256]{1,0:T(2,128)S(1)} %scatter_fusion, s32[128]{0:T(128)S(1)} %get-tuple-element.4, f32[128]{0:T(128)S(1)} %get-tuple-element.2), kind=kCustom, calls=%fused_computation.1 | custom fusion | bytes 2560 | tf_op jit(solution)/shard_map/scatter | solution.py:25
  16.2 0.1 reshape.27
  16.3 13.8 %all_to_all.20 = f32[2,8,4,8]{3,2,0,1:T(4,128)S(1)} all-to-all(f32[2,8,4,8]{3,2,0,1:T(4,128)S(1)} %copy.14), channel_id=1, replica_groups=mesh['gx'=8,'gy'=4] {'gx'}, dimensions={1} | all-to-all | bytes 4096 | tf_op jit(solution)/shard_map/all_to_all | solution.py:36
  30.1 0.0 copy-start
  30.1 0.7 reshape.56
  30.8 3.2 %all-to-all-start.1 = ((f32[4,1,128]{2,1,0:T(1,128)}), f32[4,1,128]{2,1,0:T(1,128)S(1)}, u32[]{:S(2)}, u32[]{:S(2)}) async-start(f32[4,1,128]{2,1,0:T(1,128)} %reshape.56), calls=%async_computation.1 | async-start | bytes 4096 | tf_op jit(solution)/shard_map/all_to_all | solution.py:35
  34.0 0.0 copy-done
  34.0 1.5 %scatter_custom_fusion.2 = bf16[256,128]{1,0:T(8,128)(2,1)} fusion(s32[128]{0:T(128)S(1)} %get-tuple-element.5, bf16[128,128]{1,0:T(8,128)(2,1)S(1)} %copy-done, f32[128]{0:T(128)S(1)} %copy-done.1, bf16[]{:T(256)} %constant.38.clone.1), kind=kCustom, calls=%fused_computation.11 | custom fusion | flops 49152 | bytes 98818 | tf_op jit(solution)/shard_map/scatter | solution.py:23
  35.6 2.1 %all-to-all-done.1 = f32[4,1,128]{2,1,0:T(1,128)S(1)} async-done(((f32[4,1,128]{2,1,0:T(1,128)}), f32[4,1,128]{2,1,0:T(1,128)S(1)}, u32[]{:S(2)}, u32[]{:S(2)}) %all-to-all-start.1) | async-done | bytes 2080 | tf_op jit(solution)/shard_map/all_to_all | solution.py:35
  37.7 3.3 %all-to-all-start.2 = ((bf16[8,4,8,128]{3,2,1,0:T(8,128)(2,1)}), bf16[8,4,8,128]{3,2,1,0:T(8,128)(2,1)S(1)}, u32[]{:S(2)}, u32[]{:S(2)}) async-start(bf16[8,4,8,128]{3,2,1,0:T(8,128)(2,1)} %bitcast.3), calls=%async_computation.2 | async-start | bytes 131072 | tf_op jit(solution)/shard_map/all_to_all | solution.py:29
  41.0 0.5 broadcast.119
  41.6 0.7 reduce
  42.2 0.1 reshape.57
  42.3 0.1 eq.31
  42.5 0.1 reshape.51
  42.5 0.8 fusion.11
  43.4 39.9 %psum.7 = f32[]{:T(128)} all-reduce(f32[]{:T(128)} %get-tuple-element.10), channel_id=1, replica_groups=mesh['gx'=8,'gy'=4] {'gx','gy'}, use_global_device_ids=true, to_apply=%region_6.7 | all-reduce | flops 1 | bytes 8 | tf_op jit(solution)/shard_map/psum | solution.py:48
  84.0 0.0 all-to-all-done.2
  84.0 0.6 copy.17
  84.6 3.5 %all-to-all-start.3 = ((bf16[8,4,8,128]{3,2,0,1:T(8,128)(2,1)}), bf16[8,4,8,128]{3,2,0,1:T(8,128)(2,1)S(1)}, u32[]{:S(2)}, u32[]{:S(2)}) async-start(bf16[8,4,8,128]{3,2,0,1:T(8,128)(2,1)} %copy.17), calls=%async_computation.3 | async-start | bytes 131072 | tf_op jit(solution)/shard_map/all_to_all | solution.py:28
  88.1 0.5 log_subtract_fusion
  88.7 3.6 %all-to-all-done.3 = bf16[8,4,8,128]{3,2,0,1:T(8,128)(2,1)S(1)} async-done(((bf16[8,4,8,128]{3,2,0,1:T(8,128)(2,1)}), bf16[8,4,8,128]{3,2,0,1:T(8,128)(2,1)S(1)}, u32[]{:S(2)}, u32[]{:S(2)}) %all-to-all-start.3) | async-done | bytes 65568 | tf_op jit(solution)/shard_map/all_to_all | solution.py:28
  92.3 0.8 convolution_divide_fusion
  (10 shorter events, 0.1 us)
Async XLA Ops:
  1.8 0.7 copy-start.1
  30.1 3.9 %copy-start = (bf16[128,128]{1,0:T(8,128)(2,1)S(1)}, bf16[128,128]{1,0:T(8,128)(2,1)}, u32[]{:S(2)}) copy-start(bf16[128,128]{1,0:T(8,128)(2,1)} %param.3) | copy-start | bytes 98308
  30.8 6.9 %all-to-all-start.1 = ((f32[4,1,128]{2,1,0:T(1,128)}), f32[4,1,128]{2,1,0:T(1,128)S(1)}, u32[]{:S(2)}, u32[]{:S(2)}) async-start(f32[4,1,128]{2,1,0:T(1,128)} %reshape.56), calls=%async_computation.1 | async-start | bytes 4096 | tf_op jit(solution)/shard_map/all_to_all | solution.py:35
  37.7 46.3 %all-to-all-start.2 = ((bf16[8,4,8,128]{3,2,1,0:T(8,128)(2,1)}), bf16[8,4,8,128]{3,2,1,0:T(8,128)(2,1)S(1)}, u32[]{:S(2)}, u32[]{:S(2)}) async-start(bf16[8,4,8,128]{3,2,1,0:T(8,128)(2,1)} %bitcast.3), calls=%async_computation.2 | async-start | bytes 131072 | tf_op jit(solution)/shard_map/all_to_all | solution.py:29
  84.6 7.7 %all-to-all-start.3 = ((bf16[8,4,8,128]{3,2,0,1:T(8,128)(2,1)}), bf16[8,4,8,128]{3,2,0,1:T(8,128)(2,1)S(1)}, u32[]{:S(2)}, u32[]{:S(2)}) async-start(bf16[8,4,8,128]{3,2,0,1:T(8,128)(2,1)} %copy.17), calls=%async_computation.3 | async-start | bytes 131072 | tf_op jit(solution)/shard_map/all_to_all | solution.py:28
where the time goes:
time: 93.7 us; the launch traced here: 93.1 us
  blocking collectives  53.7 us (57%)
  local copies, waits for them, and re-layouts  16.6 us (18%)
  starting transfers between devices  10.1 us (11%)
  waiting for transfers between devices  5.72 us (6%)
  other arithmetic  3.83 us (4%)
  matrix products  1.64 us (2%)
  between operations  1.49 us (2%)
    psum x1, blocking collectives, shards(): total_mass = lax.psum(jnp.sum(bin_mass), ('gx', 'gy'))  39.9 us
    all_to_all x1, blocking collectives, shards(): lax.all_to_all(tagging, 'gx', split_axis=1, concat_axis=1, tiled=True)  13.8 us
    scatter x2, local copies, waits for them, and re-layouts, shards(): tagging.at[0, slots].set(goal_weights).at[1, slots]  13.7 us
    all_to_all x1, waiting for transfers between devices, shards(): lax.all_to_all(lax.all_to_all(outgoing, 'gx', split_axis=0, concat_axis=0...  3.6 us
    all_to_all x1, starting transfers between devices, shards(): lax.all_to_all(lax.all_to_all(outgoing, 'gx', split_axis=0, concat_axis=0...  3.54 us
    all_to_all x1, starting transfers between devices, shards(): lax.all_to_all(outgoing, 'gx', split_axis=0, concat_axis=0, tiled=True)  3.35 us
    all_to_all x1, starting transfers between devices, shards(): lax.all_to_all(lax.all_to_all(tagging, 'gx', split_axis=1, concat_axis=1,...  3.22 us
    all_to_all x1, waiting for transfers between devices, shards(): lax.all_to_all(lax.all_to_all(tagging, 'gx', split_axis=1, concat_axis=1,...  2.11 us
  transfers between devices with their start and end apart: 3, of which 2 were waited for; matrix products, arithmetic and copies ran while one was open for 5% of the time, Pallas kernels for 0%

commit v1 on v0

v1 whole, which is shorter than its diff:
```python
import functools

import jax
import jax.numpy as jnp
from jax import lax
from jax.experimental import pallas as pl
from jax.experimental.pallas import tpu as pltpu
from jax.sharding import PartitionSpec as P

BINS_DEV = 64
MESH = pl.DeviceIdType.MESH


def each(count, body):
    if count <= 64:
        for k in range(count):
            body(k)
    else:
        lax.fori_loop(0, count, lambda k, c: (body(k), c)[1], 0)


def split3(x):
    hi = x.astype(jnp.bfloat16).astype(jnp.float32)
    rest = x - hi
    mid = rest.astype(jnp.bfloat16).astype(jnp.float32)
    return hi, mid, rest - mid


def kernel(across, along, stride, embed_ref, bins_ref, weights_ref, mean_ref, rarity_ref, send, recv, send_sem, recv_sem):
    n = across * along
    goals, width = embed_ref.shape
    me = lax.axis_index("gx") * along + lax.axis_index("gy")

    def device(k):
        d = lax.rem(me + k + 1, n)
        return {"gx": d // along, "gy": lax.rem(d, along)}

    barrier = pltpu.get_barrier_semaphore()
    each(n - 1, lambda k: pl.semaphore_signal(barrier, inc=1, device_id=device(k), device_id_type=MESH))

    bins_row = jnp.broadcast_to(bins_ref[...], (goals, goals))
    weights_row = jnp.broadcast_to(weights_ref[...], (goals, goals))
    bins_col = bins_row.T
    weights_col = weights_row.T
    shift = BINS_DEV.bit_length() - 1
    owners_row = lax.shift_right_logical(bins_row, shift)
    owners_col = lax.shift_right_logical(bins_col, shift)
    sub = lax.broadcasted_iota(jnp.int32, (goals, goals), 0)
    lane = lax.broadcasted_iota(jnp.int32, (goals, goals), 1)
    earlier = (owners_row == owners_col) & (sub < lane)
    place = jnp.sum(earlier.astype(jnp.float32), axis=0, keepdims=True).astype(jnp.int32)
    ahead = owners_row[:1] - me - 1
    ahead = jnp.where(ahead < 0, ahead + n, ahead)
    slot = ahead * stride + place
    rows_iota = lax.broadcasted_iota(jnp.int32, (n * stride, goals), 0)
    pick = (rows_iota == slot).astype(jnp.bfloat16)

    scaled = (weights_col[:, :width] * embed_ref[...].astype(jnp.float32)).astype(jnp.bfloat16)
    hi, mid, lo = split3(weights_col)
    offset = bins_col - owners_col * BINS_DEV
    tags = (lane == offset).astype(jnp.float32)
    for i, part in enumerate((hi, mid, lo)):
        tags = jnp.where(lane == BINS_DEV + i, part, tags)
    rows = jnp.dot(pick, scaled, preferred_element_type=jnp.float32)
    marks = jnp.dot(pick, tags.astype(jnp.bfloat16), preferred_element_type=jnp.float32)

    local = jnp.sum(weights_ref[...], axis=1, keepdims=True)
    t_hi, t_mid, t_lo = split3(local)
    lanes = lax.broadcasted_iota(jnp.int32, (1, 1, goals), 2)
    first = lax.broadcasted_iota(jnp.int32, (1, stride, goals), 1) == 0
    extra = jnp.zeros((1, stride, goals), jnp.float32)
    for i, part in enumerate((t_hi, t_mid, t_lo, jnp.ones_like(local))):
        extra = jnp.where(first & (lanes == BINS_DEV + 3 + i), part[None], extra)
    rows = rows.reshape(n, stride, width).astype(jnp.bfloat16)
    marks = (marks.reshape(n, stride, goals) + extra).astype(jnp.bfloat16)
    send[:, :, :width] = rows[: n - 1]
    send[:, :, width:] = marks[: n - 1]
    recv[n - 1, :, :width] = rows[n - 1]
    recv[n - 1, :, width:] = marks[n - 1]

    pl.semaphore_wait(barrier, n - 1)

    def start(k):
        pltpu.make_async_remote_copy(
            src_ref=send.at[k],
            dst_ref=recv.at[k],
            send_sem=send_sem,
            recv_sem=recv_sem,
            device_id=device(k),
            device_id_type=MESH,
        ).start()

    each(n - 1, start)
    landed = recv.at[pl.ds(0, n - 1)]
    pltpu.make_async_copy(landed, landed, recv_sem).wait()

    data = recv[...].astype(jnp.float32).reshape(n * stride, width + goals).astype(jnp.bfloat16)
    marks = data[:, width:]
    sums = lax.dot_general(marks, data, (((0,), (0,)), ((), ())), preferred_element_type=jnp.float32)
    gram = sums[:, width:]
    g_lane = lax.broadcasted_iota(jnp.int32, (goals, goals), 1)
    g_sub = lax.broadcasted_iota(jnp.int32, (goals, goals), 0)
    is_w_lane = (g_lane >= BINS_DEV) & (g_lane < BINS_DEV + 3)
    is_w_sub = (g_sub >= BINS_DEV) & (g_sub < BINS_DEV + 3)
    mass_col = jnp.sum(jnp.where(is_w_lane, gram, 0.0), axis=1, keepdims=True)[:BINS_DEV]
    mass_row = jnp.sum(jnp.where(is_w_sub, gram, 0.0), axis=0, keepdims=True)[:, :BINS_DEV]
    total = jnp.sum(
        jnp.where((g_lane >= BINS_DEV + 3) & (g_lane < BINS_DEV + 6), gram, 0.0)[BINS_DEV + 6 : BINS_DEV + 7],
        axis=1,
        keepdims=True,
    )
    mean_ref[...] = sums[:BINS_DEV, :width] / (mass_col + 1.0)
    rarity_ref[...] = jnp.log(total / (BINS_DEV * n)) - jnp.log(mass_row + 1.0)
    pltpu.make_async_copy(send, send, send_sem).wait()


def shards(goal_embed, goal_bins, goal_weights):
    goals, width = goal_embed.shape
    across = lax.axis_size("gx")
    along = lax.axis_size("gy")
    n = across * along
    capacity = max(2, 2 * goals // n)
    stride = -(-capacity // 8) * 8
    mean, rarity = pl.pallas_call(
        functools.partial(kernel, across, along, stride),
        out_shape=(
            jax.ShapeDtypeStruct((BINS_DEV, width), jnp.float32),
            jax.ShapeDtypeStruct((1, BINS_DEV), jnp.float32),
        ),
        in_specs=[pl.BlockSpec(memory_space=pltpu.VMEM)] * 3,
        out_specs=(pl.BlockSpec(memory_space=pltpu.VMEM),) * 2,
        scratch_shapes=[
            pltpu.VMEM((n - 1, stride, width + goals), jnp.bfloat16),
            pltpu.VMEM((n, stride, width + goals), jnp.bfloat16),
            pltpu.SemaphoreType.DMA,
            pltpu.SemaphoreType.DMA,
        ],
        compiler_params=pltpu.CompilerParams(collective_id=0, has_side_effects=True),
    )(goal_embed, goal_bins.reshape(1, goals), goal_weights.reshape(1, goals))
    return mean, rarity.reshape(BINS_DEV)


def solution(mesh):
    in_specs = (P(("gx", "gy"), None), P(("gx", "gy")), P(("gx", "gy")))
    out_specs = (P(("gx", "gy"), None), P(("gx", "gy")))
    return jax.shard_map(shards, mesh=mesh, in_specs=in_specs, out_specs=out_specs, check_vma=False)
```

time: 93.7 us -> 14.4 us (0.15)
  blocking collectives: 53.7 us -> 0 us
  local copies, waits for them, and re-layouts: 16.6 us -> 1.89 us
  Pallas kernels: 0 us -> 11.6 us
  starting transfers between devices: 10.1 us -> 0 us
  waiting for transfers between devices: 5.72 us -> 0 us
  other arithmetic: 3.83 us -> 0 us
  matrix products: 1.64 us -> 0 us
    psum x1 -> x0, blocking collectives: 39.9 us -> none  [shards(): total_mass = lax.psum(jnp.sum(bin_mass), ('gx', 'gy'))]
    all_to_all x1 -> x0, blocking collectives: 13.8 us -> none  [shards(): lax.all_to_all(tagging, 'gx', split_axis=1, concat_axis=1, tiled=True)]
    scatter x2 -> x0, local copies, waits for them, and re-layouts: 13.7 us -> none  [shards(): tagging.at[0, slots].set(goal_weights).at[1, slots]]
    pallas_call x0 -> x1, Pallas kernels: none -> 11.6 us  [shards(): pl.pallas_call(functools.partial(kernel, across, along, stride), out_shap...]
    all_to_all x3 -> x0, starting transfers between devices: 10.1 us -> none  [the longest x1 3.54 us: shards(): lax.all_to_all(lax.all_to_all(outgoing, 'gx', split_axis=0, concat_axis=0...]
    all_to_all x3 -> x0, waiting for transfers between devices: 5.72 us -> none  [the longest x1 3.6 us: shards(): lax.all_to_all(lax.all_to_all(outgoing, 'gx', split_axis=0, concat_axis=0...]
    dot_general x2 -> x0, matrix products: 1.64 us -> none  [the longest x1 0.83 us: shards(): jnp.dot(selector.astype(jnp.float32), tag_rows[0], precision=lax.Precisio...]
    scatter x1 -> x0, other arithmetic: 1.54 us -> none  [shards(): jnp.zeros((devices * capacity, width), jnp.bfloat16).at[slots].set(scaled)]
  transfers between devices with their start and end apart: 3 -> 0, of which waited for: 2 -> 0; matrix products, arithmetic and copies ran while one was open for 5% -> 0% of each run, Pallas kernels for 0% -> 0%
where the time goes in v1:
time: 14.4 us; the launch traced here: 14.1 us
  Pallas kernels  11.6 us (81%)
  local copies, waits for them, and re-layouts  1.89 us (13%)
  between operations  0.65 us (5%)
    pallas_call x1, Pallas kernels, shards(): pl.pallas_call(functools.partial(kernel, across, along, stride), out_shap...  11.6 us
    unnamed x4, local copies, waits for them, and re-layouts  1.89 us

profile of v1, /device:TPU:0, one launch (start us, length us, event | category | flops | bytes accessed | tf_op | source)
XLA Modules:
  0.0 14.1 jit_solution(4447146689650252054)
XLA Ops:
  0.6 11.6 %shard_map.50 = (f32[64,128]{1,0:T(8,128)}, f32[1,64]{1,0:T(1,128)}) custom-call(bf16[128,128]{1,0:T(8,128)(2,1)} %embed_ref.1, s32[1,128]{1,0:T(1,128)} %bitcast.3, f32[1,128]{1,0:T(1,128)} %bitcast.4), custom_call_target="tpu_custom_call" | custom-call | tf_op jit(solution)/shard_map/pallas_call | solution.py:124
  12.2 0.0 copy-start
  12.2 1.4 %copy.7 = f32[64,128]{1,0:T(8,128)} copy(f32[64,128]{1,0:T(8,128)} %get-tuple-element.8) | data formatting | bytes 65536
  13.6 0.0 copy-done
  13.6 0.5 %copy.8 = f32[64]{0:T(128)} copy(f32[64]{0:T(128)S(1)} %bitcast.5) | data formatting | bytes 512
Async XLA Ops:
  12.2 1.4 %copy-start = (f32[1,64]{1,0:T(1,128)S(1)}, f32[1,64]{1,0:T(1,128)}, u32[]{:S(2)}) copy-start(f32[1,64]{1,0:T(1,128)} %get-tuple-element.5) | copy-start | bytes 772

commit v2 on v1

--- a/solution.py
+++ b/solution.py
@@ -26,7 +26,10 @@
     return hi, mid, rest - mid
 
 
-def kernel(across, along, stride, embed_ref, bins_ref, weights_ref, mean_ref, rarity_ref, send, recv, send_sem, recv_sem):
+def kernel(across, along, stride, embed_hbm, bins_hbm, weights_hbm, mean_ref, rarity_ref, send, recv, send_sem, recv_sem, embed_ref, bins_ref, weights_ref, in_sem):
+    loads = [pltpu.make_async_copy(a, b, in_sem.at[i]) for i, (a, b) in enumerate(((bins_hbm, bins_ref), (weights_hbm, weights_ref), (embed_hbm, embed_ref)))]
+    for c in loads:
+        c.start()
     n = across * along
     goals, width = embed_ref.shape
     me = lax.axis_index("gx") * along + lax.axis_index("gy")
@@ -38,6 +41,8 @@
     barrier = pltpu.get_barrier_semaphore()
     each(n - 1, lambda k: pl.semaphore_signal(barrier, inc=1, device_id=device(k), device_id_type=MESH))
 
+    for c in loads:
+        c.wait()
     bins_row = jnp.broadcast_to(bins_ref[...], (goals, goals))
     weights_row = jnp.broadcast_to(weights_ref[...], (goals, goals))
     bins_col = bins_row.T
@@ -114,6 +119,14 @@
     pltpu.make_async_copy(send, send, send_sem).wait()
 
 
+def put(mean, rarity, mean_hbm, rarity_hbm, sem):
+    copies = [pltpu.make_async_copy(mean, mean_hbm, sem.at[0]), pltpu.make_async_copy(rarity, rarity_hbm, sem.at[1])]
+    for c in copies:
+        c.start()
+    for c in copies:
+        c.wait()
+
+
 def shards(goal_embed, goal_bins, goal_weights):
     goals, width = goal_embed.shape
     across = lax.axis_size("gx")
@@ -124,19 +137,33 @@
     mean, rarity = pl.pallas_call(
         functools.partial(kernel, across, along, stride),
         out_shape=(
-            jax.ShapeDtypeStruct((BINS_DEV, width), jnp.float32),
-            jax.ShapeDtypeStruct((1, BINS_DEV), jnp.float32),
+            pltpu.VMEM((BINS_DEV, width), jnp.float32),
+            pltpu.VMEM((1, BINS_DEV), jnp.float32),
         ),
-        in_specs=[pl.BlockSpec(memory_space=pltpu.VMEM)] * 3,
+        in_specs=[pl.BlockSpec(memory_space=pl.ANY)] * 3,
         out_specs=(pl.BlockSpec(memory_space=pltpu.VMEM),) * 2,
         scratch_shapes=[
             pltpu.VMEM((n - 1, stride, width + goals), jnp.bfloat16),
             pltpu.VMEM((n, stride, width + goals), jnp.bfloat16),
             pltpu.SemaphoreType.DMA,
             pltpu.SemaphoreType.DMA,
+            pltpu.VMEM((goals, width), jnp.bfloat16),
+            pltpu.VMEM((1, goals), jnp.int32),
+            pltpu.VMEM((1, goals), jnp.float32),
+            pltpu.SemaphoreType.DMA((3,)),
         ],
         compiler_params=pltpu.CompilerParams(collective_id=0, has_side_effects=True),
     )(goal_embed, goal_bins.reshape(1, goals), goal_weights.reshape(1, goals))
+    mean, rarity = pl.pallas_call(
+        put,
+        out_shape=(
+            jax.ShapeDtypeStruct((BINS_DEV, width), jnp.float32),
+            jax.ShapeDtypeStruct((1, BINS_DEV), jnp.float32),
+        ),
+        in_specs=[pl.BlockSpec(memory_space=pltpu.VMEM)] * 2,
+        out_specs=(pl.BlockSpec(memory_space=pl.ANY),) * 2,
+        scratch_shapes=[pltpu.SemaphoreType.DMA((2,))],
+    )(pltpu.with_memory_space_constraint(mean, pltpu.VMEM), pltpu.with_memory_space_constraint(rarity, pltpu.VMEM))
     return mean, rarity.reshape(BINS_DEV)
 
 

time: 14.4 us -> 11.9 us (0.83)
  local copies, waits for them, and re-layouts: 1.89 us -> 0 us
  Pallas kernels: 11.6 us -> 11.1 us
    unnamed x4 -> x0, local copies, waits for them, and re-layouts: 1.89 us -> none
    pallas_call x1, Pallas kernels: 11.6 us -> 10.4 us  [shards(): pl.pallas_call(functools.partial(kernel, across, along, stride), out_shap...]
    pallas_call x0 -> x1, Pallas kernels: none -> 0.64 us  [shards(): pl.pallas_call(put, out_shape=(jax.ShapeDtypeStruct((BINS_DEV, width), jn...]
where the time goes in v2:
time: 11.9 us; the launch traced here: 11.7 us
  Pallas kernels  11.1 us (93%)
  between operations  0.64 us (5%)
    pallas_call x1, Pallas kernels, shards(): pl.pallas_call(functools.partial(kernel, across, along, stride), out_shap...  10.4 us
    pallas_call x1, Pallas kernels, shards(): pl.pallas_call(put, out_shape=(jax.ShapeDtypeStruct((BINS_DEV, width), jn...  0.64 us

profile of v2, /device:TPU:0, one launch (start us, length us, event | category | flops | bytes accessed | tf_op | source)
XLA Modules:
  0.0 11.7 jit_solution(16387645494665824563)
XLA Ops:
  0.6 10.4 %shard_map.50 = (f32[64,128]{1,0:T(8,128)S(1)}, f32[1,64]{1,0:T(1,128)S(1)}) custom-call(bf16[128,128]{1,0:T(8,128)(2,1)} %embed_hbm.1, s32[1,128]{1,0:T(1,128)} %bitcast.3, f32[1,128]{1,0:T(1,128)} %bitcast.4), custom_call_target="tpu_custom_call" | custom-call | tf_op jit(solution)/shard_map/pallas_call | solution.py:137
  11.1 0.6 %shard_map.51 = (f32[64,128]{1,0:T(8,128)}, f32[1,64]{1,0:T(1,128)}) custom-call(f32[64,128]{1,0:T(8,128)S(1)} %get-tuple-element.6.mean, f32[1,64]{1,0:T(1,128)S(1)} %get-tuple-element.7.rarity), custom_call_target="tpu_custom_call" | custom-call | tf_op jit(solution)/shard_map/pallas_call | solution.py:157

commit v3 on v2

--- a/solution.py
+++ b/solution.py
@@ -56,39 +56,42 @@
     place = jnp.sum(earlier.astype(jnp.float32), axis=0, keepdims=True).astype(jnp.int32)
     ahead = owners_row[:1] - me - 1
     ahead = jnp.where(ahead < 0, ahead + n, ahead)
-    slot = ahead * stride + place
     rows_iota = lax.broadcasted_iota(jnp.int32, (n * stride, goals), 0)
-    pick = (rows_iota == slot).astype(jnp.bfloat16)
+    base = ahead * stride
+    pick = (rows_iota == base + place).astype(jnp.bfloat16)
+    group = ((rows_iota >= base) & (rows_iota < base + stride)).astype(jnp.bfloat16)
 
+    offset = bins_col - owners_col * BINS_DEV
+    place_col = jnp.sum(((owners_row == owners_col) & (lane < sub)).astype(jnp.float32), axis=1, keepdims=True)
+    hit = (lane == offset) | (lane == offset + BINS_DEV)
+    masses = jnp.zeros((n * stride, goals), jnp.float32)
+    for part in split3(weights_col):
+        spread = jnp.where(hit, part, 0.0).astype(jnp.bfloat16)
+        masses = masses + jnp.dot(group, spread, preferred_element_type=jnp.float32)
+    spot = jnp.where(lane == place_col.astype(jnp.int32) + BINS_DEV, offset.astype(jnp.float32), 0.0)
+    offsets = jnp.dot(group, spot.astype(jnp.bfloat16), preferred_element_type=jnp.float32)
+    local = jnp.sum(weights_ref[...], axis=1, keepdims=True)
+    t_lane = lax.broadcasted_iota(jnp.int32, (1, goals), 1)
+    extra = jnp.zeros((1, goals), jnp.float32)
+    for i, part in enumerate(split3(local)):
+        extra = jnp.where(t_lane == BINS_DEV + stride + i, part, extra)
+    hi, mid, lo = split3(masses)
+    low_half = lax.broadcasted_iota(jnp.int32, (n * stride, goals), 1) < BINS_DEV
+    line = lax.rem(rows_iota, stride)
+    marks = jnp.where(line == 0, jnp.where(low_half, lo, offsets + extra), jnp.where(low_half, hi, mid))
     scaled = (weights_col[:, :width] * embed_ref[...].astype(jnp.float32)).astype(jnp.bfloat16)
-    hi, mid, lo = split3(weights_col)
-    offset = bins_col - owners_col * BINS_DEV
-    tags = (lane == offset).astype(jnp.float32)
-    for i, part in enumerate((hi, mid, lo)):
-        tags = jnp.where(lane == BINS_DEV + i, part, tags)
     rows = jnp.dot(pick, scaled, preferred_element_type=jnp.float32)
-    marks = jnp.dot(pick, tags.astype(jnp.bfloat16), preferred_element_type=jnp.float32)
-
-    local = jnp.sum(weights_ref[...], axis=1, keepdims=True)
-    t_hi, t_mid, t_lo = split3(local)
-    lanes = lax.broadcasted_iota(jnp.int32, (1, 1, goals), 2)
-    first = lax.broadcasted_iota(jnp.int32, (1, stride, goals), 1) == 0
-    extra = jnp.zeros((1, stride, goals), jnp.float32)
-    for i, part in enumerate((t_hi, t_mid, t_lo, jnp.ones_like(local))):
-        extra = jnp.where(first & (lanes == BINS_DEV + 3 + i), part[None], extra)
-    rows = rows.reshape(n, stride, width).astype(jnp.bfloat16)
-    marks = (marks.reshape(n, stride, goals) + extra).astype(jnp.bfloat16)
-    send[:, :, :width] = rows[: n - 1]
-    send[:, :, width:] = marks[: n - 1]
-    recv[n - 1, :, :width] = rows[n - 1]
-    recv[n - 1, :, width:] = marks[n - 1]
+    full = jnp.concatenate([rows.reshape(n, stride, width), marks.reshape(n, stride, goals)], axis=1)
+    full = full.astype(jnp.bfloat16)
+    send[...] = full[: n - 1]
+    recv[n - 1] = full[n - 1]
 
     pl.semaphore_wait(barrier, n - 1)
 
     def start(k):
         pltpu.make_async_remote_copy(
-            src_ref=send.at[k],
-            dst_ref=recv.at[k],
+            src_ref=send.at[k, pl.ds(0, stride + 2)],
+            dst_ref=recv.at[k, pl.ds(0, stride + 2)],
             send_sem=send_sem,
             recv_sem=recv_sem,
             device_id=device(k),
@@ -96,27 +99,29 @@
         ).start()
 
     each(n - 1, start)
-    landed = recv.at[pl.ds(0, n - 1)]
+    landed = recv.at[pl.ds(0, n - 1), pl.ds(0, stride + 2)]
     pltpu.make_async_copy(landed, landed, recv_sem).wait()
 
-    data = recv[...].astype(jnp.float32).reshape(n * stride, width + goals).astype(jnp.bfloat16)
-    marks = data[:, width:]
-    sums = lax.dot_general(marks, data, (((0,), (0,)), ((), ())), preferred_element_type=jnp.float32)
-    gram = sums[:, width:]
-    g_lane = lax.broadcasted_iota(jnp.int32, (goals, goals), 1)
-    g_sub = lax.broadcasted_iota(jnp.int32, (goals, goals), 0)
-    is_w_lane = (g_lane >= BINS_DEV) & (g_lane < BINS_DEV + 3)
-    is_w_sub = (g_sub >= BINS_DEV) & (g_sub < BINS_DEV + 3)
-    mass_col = jnp.sum(jnp.where(is_w_lane, gram, 0.0), axis=1, keepdims=True)[:BINS_DEV]
-    mass_row = jnp.sum(jnp.where(is_w_sub, gram, 0.0), axis=0, keepdims=True)[:, :BINS_DEV]
+    data = recv[...].astype(jnp.float32)
+    tags = data[:, stride:]
+    s_sub = lax.broadcasted_iota(jnp.int32, (n, stride, goals), 1)
+    s_lane = lax.broadcasted_iota(jnp.int32, (n, stride, goals), 2)
+    spread = jnp.where(s_lane == s_sub + BINS_DEV, jnp.broadcast_to(tags[:, :1], (n, stride, goals)), 0.0)
+    labels = jnp.sum(spread, axis=2, keepdims=True).astype(jnp.int32)
+    choose = (s_lane == labels).astype(jnp.float32).reshape(n * stride, goals).astype(jnp.bfloat16)
+    values = data[:, :stride].reshape(n * stride, width).astype(jnp.bfloat16)
+    sums = lax.dot_general(choose, values, (((0,), (0,)), ((), ())), preferred_element_type=jnp.float32)
+    added = jnp.sum(tags, axis=0)
+    low, high = added[:1], added[1:2]
+    mass = high + pltpu.roll(high, goals - BINS_DEV, 1) + low
     total = jnp.sum(
-        jnp.where((g_lane >= BINS_DEV + 3) & (g_lane < BINS_DEV + 6), gram, 0.0)[BINS_DEV + 6 : BINS_DEV + 7],
-        axis=1,
-        keepdims=True,
+        jnp.where((t_lane >= BINS_DEV + stride) & (t_lane < BINS_DEV + stride + 3), low, 0.0), axis=1, keepdims=True
     )
-    mean_ref[...] = sums[:BINS_DEV, :width] / (mass_col + 1.0)
-    rarity_ref[...] = jnp.log(total / (BINS_DEV * n)) - jnp.log(mass_row + 1.0)
-    pltpu.make_async_copy(send, send, send_sem).wait()
+    mass_col = jnp.broadcast_to(mass, (goals, goals)).T
+    mean_ref[...] = sums[:BINS_DEV] / (mass_col[:BINS_DEV, :width] + 1.0)
+    rarity_ref[...] = jnp.log(total / (BINS_DEV * n)) - jnp.log(mass[:, :BINS_DEV] + 1.0)
+    sent = send.at[:, pl.ds(0, stride + 2)]
+    pltpu.make_async_copy(sent, sent, send_sem).wait()
 
 
 def put(mean, rarity, mean_hbm, rarity_hbm, sem):
@@ -143,8 +148,8 @@
         in_specs=[pl.BlockSpec(memory_space=pl.ANY)] * 3,
         out_specs=(pl.BlockSpec(memory_space=pltpu.VMEM),) * 2,
         scratch_shapes=[
-            pltpu.VMEM((n - 1, stride, width + goals), jnp.bfloat16),
-            pltpu.VMEM((n, stride, width + goals), jnp.bfloat16),
+            pltpu.VMEM((n - 1, 2 * stride, width), jnp.bfloat16),
+            pltpu.VMEM((n, 2 * stride, width), jnp.bfloat16),
             pltpu.SemaphoreType.DMA,
             pltpu.SemaphoreType.DMA,
             pltpu.VMEM((goals, width), jnp.bfloat16),

time: 11.9 us -> 11.5 us (0.966)
  Pallas kernels: 11.1 us -> 10.7 us
    pallas_call x1, Pallas kernels: 10.4 us -> 10 us  [shards(): pl.pallas_call(functools.partial(kernel, across, along, stride), out_shap...]
where the time goes in v3:
time: 11.5 us; the launch traced here: 11.3 us
  Pallas kernels  10.7 us (93%)
  between operations  0.64 us (6%)
    pallas_call x1, Pallas kernels, shards(): pl.pallas_call(functools.partial(kernel, across, along, stride), out_shap...  10 us
    pallas_call x1, Pallas kernels, shards(): pl.pallas_call(put, out_shape=(jax.ShapeDtypeStruct((BINS_DEV, width), jn...  0.64 us

profile of v3, /device:TPU:0, one launch (start us, length us, event | category | flops | bytes accessed | tf_op | source)
XLA Modules:
  0.0 11.3 jit_solution(14408205068196347873)
XLA Ops:
  0.6 10.0 %shard_map.50 = (f32[64,128]{1,0:T(8,128)S(1)}, f32[1,64]{1,0:T(1,128)S(1)}) custom-call(bf16[128,128]{1,0:T(8,128)(2,1)} %embed_hbm.1, s32[1,128]{1,0:T(1,128)} %bitcast.3, f32[1,128]{1,0:T(1,128)} %bitcast.4), custom_call_target="tpu_custom_call" | custom-call | tf_op jit(solution)/shard_map/pallas_call | solution.py:142
  10.7 0.6 %shard_map.51 = (f32[64,128]{1,0:T(8,128)}, f32[1,64]{1,0:T(1,128)}) custom-call(f32[64,128]{1,0:T(8,128)S(1)} %get-tuple-element.6.mean, f32[1,64]{1,0:T(1,128)S(1)} %get-tuple-element.7.rarity), custom_call_target="tpu_custom_call" | custom-call | tf_op jit(solution)/shard_map/pallas_call | solution.py:162

commit v4 on v3

--- a/solution.py
+++ b/solution.py
@@ -31,6 +31,7 @@
     for c in loads:
         c.start()
     n = across * along
+    near = n // 4
     goals, width = embed_ref.shape
     me = lax.axis_index("gx") * along + lax.axis_index("gy")
 
@@ -93,25 +94,28 @@
             src_ref=send.at[k, pl.ds(0, stride + 2)],
             dst_ref=recv.at[k, pl.ds(0, stride + 2)],
             send_sem=send_sem,
-            recv_sem=recv_sem,
+            recv_sem=recv_sem.at[jnp.int32(k >= near)],
             device_id=device(k),
             device_id_type=MESH,
         ).start()
 
     each(n - 1, start)
-    landed = recv.at[pl.ds(0, n - 1), pl.ds(0, stride + 2)]
-    pltpu.make_async_copy(landed, landed, recv_sem).wait()
-
-    data = recv[...].astype(jnp.float32)
-    tags = data[:, stride:]
-    s_sub = lax.broadcasted_iota(jnp.int32, (n, stride, goals), 1)
-    s_lane = lax.broadcasted_iota(jnp.int32, (n, stride, goals), 2)
-    spread = jnp.where(s_lane == s_sub + BINS_DEV, jnp.broadcast_to(tags[:, :1], (n, stride, goals)), 0.0)
-    labels = jnp.sum(spread, axis=2, keepdims=True).astype(jnp.int32)
-    choose = (s_lane == labels).astype(jnp.float32).reshape(n * stride, goals).astype(jnp.bfloat16)
-    values = data[:, :stride].reshape(n * stride, width).astype(jnp.bfloat16)
-    sums = lax.dot_general(choose, values, (((0,), (0,)), ((), ())), preferred_element_type=jnp.float32)
-    added = jnp.sum(tags, axis=0)
+    sums = jnp.zeros((goals, width), jnp.float32)
+    added = jnp.zeros((stride, goals), jnp.float32)
+    for group, lo_slot, hi_slot, count in ((1, near, n, n - 1 - near), (0, 0, near, near)):
+        landed = recv.at[pl.ds(lo_slot, count), pl.ds(0, stride + 2)]
+        pltpu.make_async_copy(landed, landed, recv_sem.at[group]).wait()
+        slots = hi_slot - lo_slot
+        data = recv[lo_slot:hi_slot].astype(jnp.float32)
+        tags = data[:, stride:]
+        s_sub = lax.broadcasted_iota(jnp.int32, (slots, stride, goals), 1)
+        s_lane = lax.broadcasted_iota(jnp.int32, (slots, stride, goals), 2)
+        spread = jnp.where(s_lane == s_sub + BINS_DEV, jnp.broadcast_to(tags[:, :1], (slots, stride, goals)), 0.0)
+        labels = jnp.sum(spread, axis=2, keepdims=True).astype(jnp.int32)
+        choose = (s_lane == labels).astype(jnp.float32).reshape(slots * stride, goals).astype(jnp.bfloat16)
+        values = data[:, :stride].reshape(slots * stride, width).astype(jnp.bfloat16)
+        sums = sums + lax.dot_general(choose, values, (((0,), (0,)), ((), ())), preferred_element_type=jnp.float32)
+        added = added + jnp.sum(tags, axis=0)
     low, high = added[:1], added[1:2]
     mass = high + pltpu.roll(high, goals - BINS_DEV, 1) + low
     total = jnp.sum(
@@ -151,7 +155,7 @@
             pltpu.VMEM((n - 1, 2 * stride, width), jnp.bfloat16),
             pltpu.VMEM((n, 2 * stride, width), jnp.bfloat16),
             pltpu.SemaphoreType.DMA,
-            pltpu.SemaphoreType.DMA,
+            pltpu.SemaphoreType.DMA((2,)),
             pltpu.VMEM((goals, width), jnp.bfloat16),
             pltpu.VMEM((1, goals), jnp.int32),
             pltpu.VMEM((1, goals), jnp.float32),

time: 11.5 us -> 11.5 us (level)
  no operation moved by 1% of the time
where the time goes in v4:
time: 11.5 us; the launch traced here: 11.3 us
  Pallas kernels  10.7 us (93%)
  between operations  0.64 us (6%)
    pallas_call x1, Pallas kernels, shards(): pl.pallas_call(functools.partial(kernel, across, along, stride), out_shap...  10.1 us
    pallas_call x1, Pallas kernels, shards(): pl.pallas_call(put, out_shape=(jax.ShapeDtypeStruct((BINS_DEV, width), jn...  0.64 us

profile of v4, /device:TPU:0, one launch (start us, length us, event | category | flops | bytes accessed | tf_op | source)
XLA Modules:
  0.0 11.3 jit_solution(8504402811477337241)
XLA Ops:
  0.6 10.1 %shard_map.50 = (f32[64,128]{1,0:T(8,128)S(1)}, f32[1,64]{1,0:T(1,128)S(1)}) custom-call(bf16[128,128]{1,0:T(8,128)(2,1)} %embed_hbm.1, s32[1,128]{1,0:T(1,128)} %bitcast.3, f32[1,128]{1,0:T(1,128)} %bitcast.4), custom_call_target="tpu_custom_call" | custom-call | tf_op jit(solution)/shard_map/pallas_call | solution.py:146
  10.7 0.6 %shard_map.51 = (f32[64,128]{1,0:T(8,128)}, f32[1,64]{1,0:T(1,128)}) custom-call(f32[64,128]{1,0:T(8,128)S(1)} %get-tuple-element.6.mean, f32[1,64]{1,0:T(1,128)S(1)} %get-tuple-element.7.rarity), custom_call_target="tpu_custom_call" | custom-call | tf_op jit(solution)/shard_map/pallas_call | solution.py:166
